TPU v7x, 32 devices: a whole 2x2x4 slice. The times are simulated.
32 devices in a mesh: row: 4 (over z), col: 4 (over x, core), depth: 2 (over y).
Axes of the slice: x: 2, y: 2, z: 4, core: 2. Of those that a mesh axis runs over, the one named last changes fastest.
Arguments:
- tokens: bfloat16 [2048, 8192], P(('row', 'col'), 'depth'), may hold values from -0.3125 to 0.3125
- weight: bfloat16 [8192, 8192], P('depth', ('col', 'row')), may hold values from -0.0625 to 0.0625
- grad_output: bfloat16 [2048, 8192], P('row', ('col', 'depth')), may hold values from -6 to 6
Outputs:
- grad_input: bfloat16 [2048, 8192], P(('row', 'col'), 'depth')
- grad_weight: bfloat16 [8192, 8192], P('depth', ('col', 'row'))
All inputs are finite; a program needn't handle non-finite values.
Results may differ from a plain program's by a relative error of at most 0.001.
Values may be sent and summed in bfloat16 or wider, within the bound.
A program may use at most 128 MiB of HBM per device.

v0:
```python
import jax
import jax.numpy as jnp
from jax import lax
from jax.experimental import pallas as pl
from jax.experimental.pallas import tpu as pltpu
from jax.sharding import PartitionSpec as P

last_with_last = (((1,), (1,)), ((), ()))
first_with_first = (((0,), (0,)), ((), ()))
MESH = pl.DeviceIdType.MESH
CHUNKS = 4
GROUP = 16
SPAN = 83.0
TINY = 1e-30
F32, BF16 = jnp.float32, jnp.bfloat16


def input_grads(weight, grad_block):
    weight_block = lax.all_gather(weight, "row", axis=1, tiled=True)
    partial_value = lax.dot_general(
        grad_block, weight_block, last_with_last, preferred_element_type=jnp.float32
    )
    column_slab = lax.psum_scatter(partial_value, "col", scatter_dimension=1, tiled=True).astype(
        jnp.bfloat16
    )
    return lax.all_to_all(column_slab, "col", split_axis=0, concat_axis=1, tiled=True)


def weight_grads(tokens, grad_block):
    partial_value = lax.dot_general(
        lax.all_gather(tokens, "col", axis=0, tiled=True),
        grad_block,
        first_with_first,
        preferred_element_type=jnp.float32,
    )
    return lax.psum_scatter(partial_value, "row", scatter_dimension=1, tiled=True).astype(
        jnp.bfloat16
    )


def per_device_general(tokens, weight, grad_output):
    grad_block = lax.all_gather(grad_output, "depth", axis=1, tiled=True)
    grad_input = input_grads(weight, grad_block)
    grad_weight = weight_grads(tokens, grad_block)
    return (grad_input, grad_weight)


def place(c):
    return 2 * (c % 2) + c // 2


def kernel(
    tok, w, g, gi, gw,
    g_all, g_mid, x_all, x_t, w_all, part, gw_out, gi_out, ups, upr, dns, dnr,
    g_pre, g_z, g_x, g_y, g_d, x_r, w_r, x_z, up_r, dn_r, gi_r, gw_r,
    s_pre, s_z, s_x, s_y, s_d, s_xc, s_w, s_xz, s_up, s_dn, s_gi, s_gw, l_gi, l_gw,
):
    r, c, d = lax.axis_index("row"), lax.axis_index("col"), lax.axis_index("depth")
    k, x = c % 2, c // 2
    other = 1 - d
    core = c + 1 - 2 * k
    across = c + 2 - 4 * x
    diagonal = 3 - c
    peers = (across, diagonal, core)
    tl, il = tok.shape
    tb = 4 * tl
    half = tb // 2
    ib = il // 4
    ic = ib // CHUNKS
    ol = w.shape[1]

    barrier = pltpu.get_barrier_semaphore()
    for q in peers:
        pl.semaphore_signal(barrier, inc=1, device_id={"col": q}, device_id_type=MESH)
    pl.semaphore_signal(barrier, inc=1, device_id={"depth": other}, device_id_type=MESH)
    for s in (1, 2, 3):
        pl.semaphore_signal(barrier, inc=1, device_id={"row": (r + s) % 4}, device_id_type=MESH)
    pl.semaphore_wait(barrier, 7)

    sent = []

    def when(cond, f):
        if cond is None:
            f()
        else:
            pl.when(cond)(f)

    def send(src, dst, s_sem, r_sem, to, cond=None):
        copy = pltpu.make_async_remote_copy(
            src_ref=src, dst_ref=dst, send_sem=s_sem, recv_sem=r_sem, device_id=to, device_id_type=MESH
        )
        when(cond, copy.start)
        sent.append((copy.wait_send, cond))

    def local(src, dst, sem, cond=None):
        when(cond, pltpu.make_async_copy(src, dst, sem).start)

    def arrived(ref, sem, cond=None):
        when(cond, pltpu.make_async_copy(ref, ref, sem).wait)

    def at(i, n):
        return pl.ds(pl.multiple_of(i * n, n), n)

    def g_unit(s, h, q):
        return g_all.at[at(s * 2 + h, half), at(place(q), ol)]

    for h in (0, 1):
        to = 2 * d + h
        mine = to == r
        ours = g.at[at(d, half), at(h, ol)]
        theirs = g.at[at(other, half), at(h, ol)]
        send(theirs, g_unit(r, other, c), s_pre.at[h], g_z.at[r], {"depth": other}, mine)
        send(theirs, g_mid.at[h], s_pre.at[h], g_pre.at[h], {"depth": other}, jnp.logical_not(mine))
        local(ours, g_unit(r, d, c), g_z.at[r], mine)
        send(ours, g_unit(r, d, c), s_z.at[h], g_z.at[r], {"row": to}, jnp.logical_not(mine))

    def send_tokens(j):
        for i, q in enumerate(peers):
            send(
                tok.at[:, at(q * CHUNKS + j, ic)], x_all.at[j, at(r * 4 + c, tl)],
                s_xc.at[j, i], x_r.at[j, c], {"col": q},
            )
        local(tok.at[:, at(c * CHUNKS + j, ic)], x_all.at[j, at(r * 4 + c, tl)], x_r.at[j, c])

    def send_weight(j):
        for i, q in enumerate(peers):
            send(
                w.at[at(q * CHUNKS + j, ic)], w_all.at[j, :, at(place(c), ol)],
                s_w.at[j, i], w_r.at[j, c], {"col": q},
            )
        local(w.at[at(c * CHUNKS + j, ic)], w_all.at[j, :, at(place(c), ol)], w_r.at[j, c])

    for j in range(CHUNKS):
        send_tokens(j)
    send_weight(0)

    def tokens_on(j, s, direction, cond):
        block = x_all.at[j, at(s, tb)]
        send(block, block, s_xz.at[j, direction, s], x_z.at[j, s], {"row": r + 1 - 2 * direction}, cond)

    up_ok, down_ok = r < 3, r > 0

    def own_tokens_on(j):
        for q in range(4):
            arrived(x_all.at[j, at(r * 4 + q, tl)], x_r.at[j, q])
        tokens_on(j, r, 0, up_ok)
        tokens_on(j, r, 1, down_ok)

    def pass_tokens(j, far):
        below, above = r - far, r + far
        low, high = jnp.maximum(below, 0), jnp.minimum(above, 3)
        has_low, has_high = below >= 0, above <= 3
        arrived(x_all.at[j, at(low, tb)], x_z.at[j, low], has_low)
        tokens_on(j, low, 0, jnp.logical_and(has_low, up_ok))
        arrived(x_all.at[j, at(high, tb)], x_z.at[j, high], has_high)
        tokens_on(j, high, 1, jnp.logical_and(has_high, down_ok))

    order = [(r, None)]
    for far in (1, 2, 3):
        order.append((jnp.maximum(r - far, 0), r - far >= 0))
        order.append((jnp.minimum(r + far, 3), r + far <= 3))

    def spread(s, cond):
        unit = g_unit(s, d, c)
        arrived(unit, g_z.at[s], cond)
        send(unit, unit, s_x.at[s], g_x.at[s], {"col": across}, cond)
        send(unit, unit, s_y.at[0, s], g_y.at[0, s], {"depth": other}, cond)

    def spread_crossed(s, cond):
        unit = g_unit(s, d, across)
        arrived(unit, g_x.at[s], cond)
        send(unit, unit, s_y.at[1, s], g_y.at[1, s], {"depth": other}, cond)

    def to_core(s, cond):
        arrived(g_unit(s, other, c), g_y.at[0, s], cond)
        arrived(g_unit(s, other, across), g_y.at[1, s], cond)
        slab = g_all.at[at(s, tb), at(k, 2 * ol)]
        send(slab, slab, s_d.at[s], g_d.at[s], {"col": core}, cond)

    own_tokens_on(0)
    own_tokens_on(1)
    for h in (0, 1):
        to = 2 * other + h
        go = to != r
        arrived(g_mid.at[h], g_pre.at[h], go)
        send(g_mid.at[h], g_unit(r, d, c), s_z.at[2 + h], g_z.at[r], {"row": to}, go)
    spread(*order[0])
    own_tokens_on(2)
    own_tokens_on(3)
    spread(*order[1])
    spread(*order[2])
    pass_tokens(0, 1)
    spread(*order[3])
    spread(*order[4])
    pass_tokens(1, 1)
    spread(*order[5])
    spread(*order[6])
    for j in range(1, CHUNKS):
        send_weight(j)
    pass_tokens(2, 1)
    pass_tokens(3, 1)
    for n, (s, cond) in enumerate(order):
        spread_crossed(s, cond)
        if n >= 3:
            pass_tokens(n - 3, 2)
    for s, cond in order:
        to_core(s, cond)
    for s in range(4):
        arrived(g_all.at[at(s, tb), at(1 - k, 2 * ol)], g_d.at[s])

    def multiply_input(j):
        for q in range(4):
            arrived(w_all.at[j, :, at(place(q), ol)], w_r.at[j, q])

        def body(b, carry):
            rows = at(b, tb)
            part[j, rows, :] = lax.dot_general(
                g_all[rows, :], w_all[j], last_with_last, preferred_element_type=F32
            )
            return carry

        lax.fori_loop(0, 4, body, None)

    def multiply_weight(j):
        def turn(b, carry):
            x_t[:, at(b, half)] = x_all[j, at(b, half), :].T
            return carry

        lax.fori_loop(0, 8, turn, None)

        def body(n, carry):
            cols = at(n, ol)
            gw_out[j, :, cols] = jnp.dot(
                x_t[...], g_all[:, cols], preferred_element_type=F32
            ).astype(BF16)
            return carry

        lax.fori_loop(0, 4, body, None)
        for i, q in enumerate(peers):
            send(
                gw_out.at[j, :, at(place(q), ol)], gw.at[at(c * CHUNKS + j, ic)],
                s_gw.at[j, i], gw_r.at[j, c], {"col": q},
            )
        local(gw_out.at[j, :, at(place(c), ol)], gw.at[at(c * CHUNKS + j, ic)], l_gw.at[j])

    step = 64
    scale_rows = pl.ds(tb, GROUP)

    def read_code(buf, i, rows, unit):
        v = buf[i, rows, :].astype(F32)
        size = jnp.log(jnp.abs(v)) + SPAN
        size = size * jnp.concatenate([unit] * (step // GROUP), axis=0)
        return jnp.where(v < 0, -size, size)

    def unit_of(buf, i):
        return buf[i, scale_rows, :].astype(F32) * (0.5 / SPAN)

    def encode(j, b, out, slot, got):
        unit = None if got is None else unit_of(got, slot)

        def total(t):
            value = part[j, pl.ds(pl.multiple_of(b * tb + t * step, step), step), :]
            if got is not None:
                value = value + read_code(got, slot, at(t, step), unit)
            return value

        def first(t, most):
            value = total(t)
            if got is not None:
                part[j, pl.ds(pl.multiple_of(b * tb + t * step, step), step), :] = value
            size = jnp.abs(value)
            for n in range(step // GROUP):
                most = jnp.maximum(most, size[n * GROUP : (n + 1) * GROUP])
            return most

        most = lax.fori_loop(0, tb // step, first, jnp.full((GROUP, ic), TINY, F32))
        scale = (most * 1.01).astype(BF16)
        out[slot, scale_rows, :] = scale
        by = (2 * SPAN) / scale.astype(F32)
        by = jnp.concatenate([by] * (step // GROUP), axis=0)

        def second(t, carry):
            value = part[j, pl.ds(pl.multiple_of(b * tb + t * step, step), step), :]
            code = jnp.exp(jnp.abs(value) * by - SPAN)
            out[slot, at(t, step), :] = jnp.where(value < 0, -code, code).astype(BF16)
            return carry

        lax.fori_loop(0, tb // step, second, None)

    def add_in(j, got, slot):
        unit = unit_of(got, slot)

        def body(t, carry):
            rows = pl.ds(pl.multiple_of(r * tb + t * step, step), step)
            part[j, rows, :] = part[j, rows, :] + read_code(got, slot, at(t, step), unit)
            return carry

        lax.fori_loop(0, tb // step, body, None)

    def ring(j, level, up):
        here = level if up else 3 - level
        out, got, s_sem, r_sem = (ups, upr, s_up, up_r) if up else (dns, dnr, s_dn, dn_r)
        toward = {"row": r + 1 if up else r - 1}
        far = [3, 2, 1, 0] if up else [0, 1, 2, 3]

        def slot_of(b):
            return j * 3 + (b - 1 if up else b)

        copies = []
        for b in far[: 3 - level]:
            i = slot_of(b)
            copies.append(
                (b, i, pltpu.make_async_remote_copy(
                    src_ref=out.at[i], dst_ref=got.at[i], send_sem=s_sem.at[i], recv_sem=r_sem.at[i],
                    device_id=toward, device_id_type=MESH,
                ))
            )
        cond = r == here

        @pl.when(cond)
        def _():
            for b, i, copy in copies:
                if level > 0:
                    arrived(got.at[i], r_sem.at[i])
                encode(j, b, out, i, got if level > 0 else None)
                copy.start()
            if level > 0:
                i = slot_of(here)
                arrived(got.at[i], r_sem.at[i])
                add_in(j, got, i)

        for _, _, copy in copies:
            sent.append((copy.wait_send, cond))

    def level(j, n):
        ring(j, n, True)
        ring(j, n, False)

    def finish(j, cond):
        @pl.when(cond)
        def _():
            gi_out[j] = part[j, at(r, tb), :].astype(BF16)

        for i, q in enumerate(peers):
            send(
                gi_out.at[j, at(q, tl)], gi.at[:, at(c * CHUNKS + j, ic)],
                s_gi.at[j, i], gi_r.at[j, c], {"col": q}, cond,
            )
        local(gi_out.at[j, at(c, tl)], gi.at[:, at(c * CHUNKS + j, ic)], l_gi.at[j], cond)

    inner = jnp.logical_or(r == 1, r == 2)
    outer = jnp.logical_or(r == 0, r == 3)

    multiply_input(0)
    level(0, 0)
    multiply_input(1)
    level(1, 0)
    level(0, 1)
    pass_tokens(0, 3)
    multiply_weight(0)
    multiply_input(2)
    level(2, 0)
    level(1, 1)
    level(0, 2)
    finish(0, inner)
    pass_tokens(1, 3)
    multiply_weight(1)
    multiply_input(3)
    level(3, 0)
    level(2, 1)
    level(1, 2)
    finish(1, inner)
    level(0, 3)
    finish(0, outer)
    pass_tokens(2, 3)
    multiply_weight(2)
    level(3, 1)
    level(2, 2)
    finish(2, inner)
    level(1, 3)
    finish(1, outer)
    pass_tokens(3, 3)
    multiply_weight(3)
    level(3, 2)
    finish(3, inner)
    level(2, 3)
    finish(2, outer)
    level(3, 3)
    finish(3, outer)

    for wait, cond in sent:
        when(cond, wait)
    for j in range(CHUNKS):
        arrived(gi.at[:, at(c * CHUNKS + j, ic)], l_gi.at[j])
        arrived(gw.at[at(c * CHUNKS + j, ic)], l_gw.at[j])
        for q in peers:
            arrived(gi.at[:, at(q * CHUNKS + j, ic)], gi_r.at[j, q])
            arrived(gw.at[at(q * CHUNKS + j, ic)], gw_r.at[j, q])


def per_device_kernel(tokens, weight, grad_output):
    tl, il = tokens.shape
    ol = weight.shape[1]
    tb, ic = 4 * tl, il // (4 * CHUNKS)
    dma = pltpu.SemaphoreType.DMA
    code = pltpu.VMEM((3 * CHUNKS, tb + GROUP, ic), BF16)
    anywhere = pl.BlockSpec(memory_space=pl.ANY)
    return pl.pallas_call(
        kernel,
        out_shape=(
            jax.ShapeDtypeStruct(tokens.shape, BF16),
            jax.ShapeDtypeStruct(weight.shape, BF16),
        ),
        in_specs=[anywhere] * 3,
        out_specs=(anywhere, anywhere),
        scratch_shapes=[
            pltpu.VMEM((4 * tb, 4 * ol), BF16),
            pltpu.VMEM((2, tb // 2, ol), BF16),
            pltpu.VMEM((CHUNKS, 4 * tb, ic), BF16),
            pltpu.VMEM((ic, 4 * tb), BF16),
            pltpu.VMEM((CHUNKS, ic, 4 * ol), BF16),
            pltpu.VMEM((CHUNKS, 4 * tb, ic), F32),
            pltpu.VMEM((CHUNKS, ic, 4 * ol), BF16),
            pltpu.VMEM((CHUNKS, tb, ic), BF16),
            code, code, code, code,
            dma((2,)), dma((4,)), dma((4,)), dma((2, 4)), dma((4,)),
            dma((CHUNKS, 4)), dma((CHUNKS, 4)), dma((CHUNKS, 4)),
            dma((3 * CHUNKS,)), dma((3 * CHUNKS,)), dma((CHUNKS, 4)), dma((CHUNKS, 4)),
            dma((2,)), dma((4,)), dma((4,)), dma((2, 4)), dma((4,)),
            dma((CHUNKS, 3)), dma((CHUNKS, 3)), dma((CHUNKS, 2, 4)),
            dma((3 * CHUNKS,)), dma((3 * CHUNKS,)), dma((CHUNKS, 3)), dma((CHUNKS, 3)),
            dma((CHUNKS,)), dma((CHUNKS,)),
        ],
        compiler_params=pltpu.CompilerParams(
            collective_id=0, has_side_effects=True, vmem_limit_bytes=62 * 2**20
        ),
    )(tokens, weight, grad_output)


def solution(mesh):
    fours_fit = mesh.shape["row"] == 4 and mesh.shape["col"] == 4 and mesh.shape["depth"] == 2
    return jax.shard_map(
        per_device_kernel if fours_fit else per_device_general,
        mesh=mesh,
        in_specs=(
            P(("row", "col"), "depth"),
            P("depth", ("col", "row")),
            P("row", ("col", "depth")),
        ),
        out_specs=(P(("row", "col"), "depth"), P("depth", ("col", "row"))),
        check_vma=False,
    )
```

profile of v0, /device:TPU:21, one launch (start us, length us, event | category | flops | bytes accessed | tf_op | source)
XLA Modules:
  0.0 184.0 jit_solution(134522205386135386)
XLA Ops:
  0.6 176.6 %shard_map.50 = (bf16[128,4096]{1,0:T(8,128)(2,1)}, bf16[4096,512]{1,0:T(8,128)(2,1)}) custom-call(bf16[128,4096]{1,0:T(8,128)(2,1)} %tok.1, bf16[4096,512]{1,0:T(8,128)(2,1)} %w.1, bf16[512,1024]{1,0:T(8,128)(2,1)} %g.1), custom_call_target="tpu_custom_call" | custom-call | tf_op jit(solution)/shard_map/pallas_call | solution.py:408
  177.3 2.3 %copy.7 = bf16[128,4096]{1,0:T(8,128)(2,1)} copy(bf16[128,4096]{1,0:T(8,128)(2,1)} %get-tuple-element.4) | data formatting | bytes 2097152
  179.5 4.5 %copy.8 = bf16[4096,512]{1,0:T(8,128)(2,1)} copy(bf16[4096,512]{1,0:T(8,128)(2,1)} %get-tuple-element.5) | data formatting | bytes 8388608
where the time goes:
time: 184 us
  Pallas kernels  177 us (96%)
  local copies, waits for them, and re-layouts  6.76 us (4%)
    pallas_call x1, Pallas kernels, per_device_kernel(): pl.pallas_call(kernel, out_shape=(jax.ShapeDtypeStruct(tokens.shape, BF16...  177 us
    unnamed x2, local copies, waits for them, and re-layouts  6.76 us

commit v1 on v0

--- a/solution.py
+++ b/solution.py
@@ -155,68 +155,53 @@
         arrived(x_all.at[j, at(high, tb)], x_z.at[j, high], has_high)
         tokens_on(j, high, 1, jnp.logical_and(has_high, down_ok))
 
-    order = [(r, None)]
-    for far in (1, 2, 3):
-        order.append((jnp.maximum(r - far, 0), r - far >= 0))
-        order.append((jnp.minimum(r + far, 3), r + far <= 3))
-
-    def spread(s, cond):
+    near = 3 * (1 - r // 2)
+    last = 1 + r % 2
+    order = [near, 6 - r - near - last, last, r]
+
+    def spread(n):
+        s = order[n]
         unit = g_unit(s, d, c)
-        arrived(unit, g_z.at[s], cond)
-        send(unit, unit, s_x.at[s], g_x.at[s], {"col": across}, cond)
-        send(unit, unit, s_y.at[0, s], g_y.at[0, s], {"depth": other}, cond)
-
-    def spread_crossed(s, cond):
+        arrived(unit, g_z.at[s])
+        send(unit, unit, s_x.at[s], g_x.at[s], {"col": across})
+        send(unit, unit, s_y.at[0, s], g_y.at[0, s], {"depth": other})
+
+    def crossed(n):
+        s = order[n]
         unit = g_unit(s, d, across)
-        arrived(unit, g_x.at[s], cond)
-        send(unit, unit, s_y.at[1, s], g_y.at[1, s], {"depth": other}, cond)
-
-    def to_core(s, cond):
-        arrived(g_unit(s, other, c), g_y.at[0, s], cond)
-        arrived(g_unit(s, other, across), g_y.at[1, s], cond)
+        arrived(unit, g_x.at[s])
+        send(unit, unit, s_y.at[1, s], g_y.at[1, s], {"depth": other})
+
+    def to_core(n):
+        s = order[n]
+        arrived(g_unit(s, other, c), g_y.at[0, s])
+        arrived(g_unit(s, other, across), g_y.at[1, s])
         slab = g_all.at[at(s, tb), at(k, 2 * ol)]
-        send(slab, slab, s_d.at[s], g_d.at[s], {"col": core}, cond)
-
-    own_tokens_on(0)
-    own_tokens_on(1)
-    for h in (0, 1):
+        send(slab, slab, s_d.at[s], g_d.at[s], {"col": core})
+
+    def pass_mid(h):
         to = 2 * other + h
         go = to != r
         arrived(g_mid.at[h], g_pre.at[h], go)
         send(g_mid.at[h], g_unit(r, d, c), s_z.at[2 + h], g_z.at[r], {"row": to}, go)
-    spread(*order[0])
-    own_tokens_on(2)
-    own_tokens_on(3)
-    spread(*order[1])
-    spread(*order[2])
-    pass_tokens(0, 1)
-    spread(*order[3])
-    spread(*order[4])
-    pass_tokens(1, 1)
-    spread(*order[5])
-    spread(*order[6])
-    for j in range(1, CHUNKS):
-        send_weight(j)
-    pass_tokens(2, 1)
-    pass_tokens(3, 1)
-    for n, (s, cond) in enumerate(order):
-        spread_crossed(s, cond)
-        if n >= 3:
-            pass_tokens(n - 3, 2)
-    for s, cond in order:
-        to_core(s, cond)
-    for s in range(4):
+
+    def from_core(n):
+        s = order[n]
         arrived(g_all.at[at(s, tb), at(1 - k, 2 * ol)], g_d.at[s])
 
-    def multiply_input(j):
+    def weight_in(j):
         for q in range(4):
             arrived(w_all.at[j, :, at(place(q), ol)], w_r.at[j, q])
 
+    def multiply_block(j, s):
+        rows = at(s, tb)
+        part[j, rows, :] = lax.dot_general(
+            g_all[rows, :], w_all[j], last_with_last, preferred_element_type=F32
+        )
+
+    def multiply_input(j):
         def body(b, carry):
-            rows = at(b, tb)
-            part[j, rows, :] = lax.dot_general(
-                g_all[rows, :], w_all[j], last_with_last, preferred_element_type=F32
-            )
+            multiply_block(j, b)
             return carry
 
         lax.fori_loop(0, 4, body, None)
@@ -297,44 +282,41 @@
 
         lax.fori_loop(0, tb // step, body, None)
 
-    def ring(j, level, up):
+    def ring(j, level, up, which):
         here = level if up else 3 - level
         out, got, s_sem, r_sem = (ups, upr, s_up, up_r) if up else (dns, dnr, s_dn, dn_r)
         toward = {"row": r + 1 if up else r - 1}
         far = [3, 2, 1, 0] if up else [0, 1, 2, 3]
-
-        def slot_of(b):
-            return j * 3 + (b - 1 if up else b)
-
-        copies = []
-        for b in far[: 3 - level]:
-            i = slot_of(b)
-            copies.append(
-                (b, i, pltpu.make_async_remote_copy(
-                    src_ref=out.at[i], dst_ref=got.at[i], send_sem=s_sem.at[i], recv_sem=r_sem.at[i],
-                    device_id=toward, device_id_type=MESH,
-                ))
+        cond = r == here
+        for n in which:
+            b = far[n]
+            i = j * 3 + (b - 1 if up else b)
+            if b == here:
+
+                @pl.when(cond)
+                def _():
+                    arrived(got.at[i], r_sem.at[i])
+                    add_in(j, got, i)
+
+                continue
+            copy = pltpu.make_async_remote_copy(
+                src_ref=out.at[i], dst_ref=got.at[i], send_sem=s_sem.at[i], recv_sem=r_sem.at[i],
+                device_id=toward, device_id_type=MESH,
             )
-        cond = r == here
-
-        @pl.when(cond)
-        def _():
-            for b, i, copy in copies:
+
+            @pl.when(cond)
+            def _():
                 if level > 0:
                     arrived(got.at[i], r_sem.at[i])
                 encode(j, b, out, i, got if level > 0 else None)
                 copy.start()
-            if level > 0:
-                i = slot_of(here)
-                arrived(got.at[i], r_sem.at[i])
-                add_in(j, got, i)
-
-        for _, _, copy in copies:
+
             sent.append((copy.wait_send, cond))
 
-    def level(j, n):
-        ring(j, n, True)
-        ring(j, n, False)
+    def level(j, n, which=None):
+        which = range(4 - n if n else 3) if which is None else which
+        ring(j, n, True, which)
+        ring(j, n, False, which)
 
     def finish(j, cond):
         @pl.when(cond)
@@ -351,51 +333,108 @@
     inner = jnp.logical_or(r == 1, r == 2)
     outer = jnp.logical_or(r == 0, r == 3)
 
-    multiply_input(0)
-    level(0, 0)
-    multiply_input(1)
-    level(1, 0)
-    level(0, 1)
-    pass_tokens(0, 3)
-    multiply_weight(0)
-    multiply_input(2)
-    level(2, 0)
-    level(1, 1)
-    level(0, 2)
-    finish(0, inner)
-    pass_tokens(1, 3)
-    multiply_weight(1)
-    multiply_input(3)
-    level(3, 0)
-    level(2, 1)
-    level(1, 2)
-    finish(1, inner)
-    level(0, 3)
-    finish(0, outer)
-    pass_tokens(2, 3)
-    multiply_weight(2)
-    level(3, 1)
-    level(2, 2)
-    finish(2, inner)
-    level(1, 3)
-    finish(1, outer)
-    pass_tokens(3, 3)
-    multiply_weight(3)
-    level(3, 2)
-    finish(3, inner)
-    level(2, 3)
-    finish(2, outer)
-    level(3, 3)
-    finish(3, outer)
-
-    for wait, cond in sent:
-        when(cond, wait)
+    def run(name, f, *args):
+        with jax.named_scope(name):
+            f(*args)
+
+    def mi(j):
+        run("w_in%d" % j, weight_in, j)
+        run("input%d" % j, multiply_input, j)
+
+    def mw(j):
+        run("pass%d_3" % j, pass_tokens, j, 3)
+        run("weight%d" % j, multiply_weight, j)
+
+    def lv(j, n, which=None):
+        run("level%d_%d" % (j, n), level, j, n, which)
+
+    def end(j, cond, name):
+        run("end%d_%s" % (j, name), finish, j, cond)
+
+    def block(n):
+        run("from_core%d" % n, from_core, n)
+        run("block%d" % n, multiply_block, 0, order[n])
+        if n < 3:
+            run("first%d" % n, level, 0, 0, [n])
+
+    def ps(j, far):
+        run("pass%d_%d" % (j, far), pass_tokens, j, far)
+
+    run("mid0", pass_mid, 0)
+    run("mid1", pass_mid, 1)
     for j in range(CHUNKS):
-        arrived(gi.at[:, at(c * CHUNKS + j, ic)], l_gi.at[j])
-        arrived(gw.at[at(c * CHUNKS + j, ic)], l_gw.at[j])
-        for q in peers:
-            arrived(gi.at[:, at(q * CHUNKS + j, ic)], gi_r.at[j, q])
-            arrived(gw.at[at(q * CHUNKS + j, ic)], gw_r.at[j, q])
+        run("own%d" % j, own_tokens_on, j)
+    run("spread3", spread, 3)
+    for n in range(3):
+        run("spread%d" % n, spread, n)
+    for j in range(1, CHUNKS):
+        send_weight(j)
+    run("crossed0", crossed, 0)
+    ps(0, 1)
+    run("crossed1", crossed, 1)
+    run("to_core0", to_core, 0)
+    ps(1, 1)
+    run("crossed2", crossed, 2)
+    run("crossed3", crossed, 3)
+    run("w_in0", weight_in, 0)
+    block(0)
+    run("to_core1", to_core, 1)
+    ps(2, 1)
+    block(1)
+    run("to_core2", to_core, 2)
+    ps(3, 1)
+    block(2)
+    run("to_core3", to_core, 3)
+    ps(0, 2)
+    block(3)
+    ps(1, 2)
+    mi(1)
+    lv(1, 0)
+    ps(2, 2)
+    lv(0, 1)
+    mw(0)
+    mi(2)
+    lv(2, 0)
+    ps(3, 2)
+    lv(0, 2)
+    end(0, inner, "in")
+    lv(1, 1)
+    mi(3)
+    lv(3, 0)
+    mw(1)
+    lv(0, 3)
+    end(0, outer, "out")
+    lv(1, 2)
+    end(1, inner, "in")
+    mw(2)
+    lv(2, 1)
+    lv(1, 3)
+    end(1, outer, "out")
+    lv(2, 2)
+    end(2, inner, "in")
+    mw(3)
+    lv(3, 1)
+    lv(2, 3)
+    end(2, outer, "out")
+    lv(3, 2)
+    end(3, inner, "in")
+    lv(3, 3)
+    end(3, outer, "out")
+
+    def drain():
+        for wait, cond in sent:
+            when(cond, wait)
+
+    def outputs():
+        for j in range(CHUNKS):
+            arrived(gi.at[:, at(c * CHUNKS + j, ic)], l_gi.at[j])
+            arrived(gw.at[at(c * CHUNKS + j, ic)], l_gw.at[j])
+            for q in peers:
+                arrived(gi.at[:, at(q * CHUNKS + j, ic)], gi_r.at[j, q])
+                arrived(gw.at[at(q * CHUNKS + j, ic)], gw_r.at[j, q])
+
+    run("drain", drain)
+    run("outputs", outputs)
 
 
 def per_device_kernel(tokens, weight, grad_output):

time: 184 us -> 154 us (0.84)
  Pallas kernels: 177 us -> 147 us
    pallas_call x1, Pallas kernels: 177 us -> 147 us  [per_device_kernel(): pl.pallas_call(kernel, out_shape=(jax.ShapeDtypeStruct(tokens.shape, BF16...]
where the time goes in v1:
time: 154 us
  Pallas kernels  147 us (95%)
  local copies, waits for them, and re-layouts  6.76 us (4%)
    pallas_call x1, Pallas kernels, per_device_kernel(): pl.pallas_call(kernel, out_shape=(jax.ShapeDtypeStruct(tokens.shape, BF16...  147 us
    unnamed x2, local copies, waits for them, and re-layouts  6.76 us

profile of v1, /device:TPU:21, one launch (start us, length us, event | category | flops | bytes accessed | tf_op | source)
XLA Modules:
  0.0 154.2 jit_solution(6415433956318296005)
XLA Ops:
  0.6 146.8 %shard_map.50 = (bf16[128,4096]{1,0:T(8,128)(2,1)}, bf16[4096,512]{1,0:T(8,128)(2,1)}) custom-call(bf16[128,4096]{1,0:T(8,128)(2,1)} %tok.1, bf16[4096,512]{1,0:T(8,128)(2,1)} %w.1, bf16[512,1024]{1,0:T(8,128)(2,1)} %g.1), custom_call_target="tpu_custom_call" | custom-call | tf_op jit(solution)/shard_map/pallas_call | solution.py:447
  147.4 2.3 %copy.7 = bf16[128,4096]{1,0:T(8,128)(2,1)} copy(bf16[128,4096]{1,0:T(8,128)(2,1)} %get-tuple-element.4) | data formatting | bytes 2097152
  149.7 4.5 %copy.8 = bf16[4096,512]{1,0:T(8,128)(2,1)} copy(bf16[4096,512]{1,0:T(8,128)(2,1)} %get-tuple-element.5) | data formatting | bytes 8388608

commit v2 on v1

--- a/solution.py
+++ b/solution.py
@@ -471,9 +471,9 @@
             dma((CHUNKS,)), dma((CHUNKS,)),
         ],
         compiler_params=pltpu.CompilerParams(
-            collective_id=0, has_side_effects=True, vmem_limit_bytes=62 * 2**20
+            collective_id=0, has_side_effects=True, vmem_limit_bytes=46 * 2**20
         ),
-    )(tokens, weight, grad_output)
+    )(*[pltpu.with_memory_space_constraint(a, pltpu.HBM) for a in (tokens, weight, grad_output)])
 
 
 def solution(mesh):

time: 154 us -> 150 us (0.974)
  local copies, waits for them, and re-layouts: 6.76 us -> 2.99 us
    unnamed x2, local copies, waits for them, and re-layouts: 6.76 us -> 2.99 us
where the time goes in v2:
time: 150 us
  Pallas kernels  147 us (98%)
  local copies, waits for them, and re-layouts  2.99 us (2%)
    pallas_call x1, Pallas kernels, per_device_kernel(): pl.pallas_call(kernel, out_shape=(jax.ShapeDtypeStruct(tokens.shape, BF16...  147 us

profile of v2, /device:TPU:21, one launch (start us, length us, event | category | flops | bytes accessed | tf_op | source)
XLA Modules:
  0.0 150.3 jit_solution(7643207866694310964)
XLA Ops:
  0.6 146.7 %shard_map.50 = (bf16[128,4096]{1,0:T(8,128)(2,1)S(1)}, bf16[4096,512]{1,0:T(8,128)(2,1)S(1)}) custom-call(bf16[128,4096]{1,0:T(8,128)(2,1)} %tok.1, bf16[4096,512]{1,0:T(8,128)(2,1)} %w.1, bf16[512,1024]{1,0:T(8,128)(2,1)} %g.1), custom_call_target="tpu_custom_call" | custom-call | tf_op jit(solution)/shard_map/pallas_call | solution.py:447
  147.3 1.0 copy.7
  148.3 2.0 %copy.8 = bf16[4096,512]{1,0:T(8,128)(2,1)} copy(bf16[4096,512]{1,0:T(8,128)(2,1)S(1)} %get-tuple-element.5) | data formatting | bytes 8388608

commit v3 on v2

--- a/solution.py
+++ b/solution.py
@@ -53,7 +53,7 @@
     tok, w, g, gi, gw,
     g_all, g_mid, x_all, x_t, w_all, part, gw_out, gi_out, ups, upr, dns, dnr,
     g_pre, g_z, g_x, g_y, g_d, x_r, w_r, x_z, up_r, dn_r, gi_r, gw_r,
-    s_pre, s_z, s_x, s_y, s_d, s_xc, s_w, s_xz, s_up, s_dn, s_gi, s_gw, l_gi, l_gw,
+    s_pre, s_z, s_x, s_y, s_d, s_xc, s_w, s_xz, s_up, s_dn, s_gi, s_gw, l_gi, l_gw, come,
 ):
     r, c, d = lax.axis_index("row"), lax.axis_index("col"), lax.axis_index("depth")
     k, x = c % 2, c // 2
@@ -69,21 +69,46 @@
     ic = ib // CHUNKS
     ol = w.shape[1]
 
-    barrier = pltpu.get_barrier_semaphore()
-    for q in peers:
-        pl.semaphore_signal(barrier, inc=1, device_id={"col": q}, device_id_type=MESH)
-    pl.semaphore_signal(barrier, inc=1, device_id={"depth": other}, device_id_type=MESH)
-    for s in (1, 2, 3):
-        pl.semaphore_signal(barrier, inc=1, device_id={"row": (r + s) % 4}, device_id_type=MESH)
-    pl.semaphore_wait(barrier, 7)
-
-    sent = []
+    up_ok, down_ok = r < 3, r > 0
+    inner, outer = jnp.logical_and(up_ok, down_ok), jnp.logical_or(r == 0, r == 3)
+
+    def tell(sem, to, cond=None):
+        when(cond, lambda: pl.semaphore_signal(sem, inc=1, device_id=to, device_id_type=MESH))
 
     def when(cond, f):
         if cond is None:
             f()
         else:
             pl.when(cond)(f)
+
+    barrier = pltpu.get_barrier_semaphore()
+    for q in peers:
+        tell(barrier, {"col": q})
+    tell(barrier, {"depth": other})
+    tell(barrier, {"row": r + 1}, up_ok)
+    tell(barrier, {"row": r - 1}, down_ok)
+    when(inner, lambda: pl.semaphore_wait(barrier, 6))
+    when(outer, lambda: pl.semaphore_wait(barrier, 5))
+    tell(come.at[0], {"row": r + 1}, inner)
+    tell(come.at[1], {"row": r - 1}, inner)
+
+    def all_in():
+        @pl.when(r >= 2)
+        def _():
+            pl.semaphore_wait(come.at[0], 1)
+
+        @pl.when(r <= 1)
+        def _():
+            pl.semaphore_wait(come.at[1], 1)
+
+        tell(come.at[2], {"row": r + 1}, r == 2)
+        tell(come.at[2], {"row": r - 1}, r == 1)
+
+        @pl.when(outer)
+        def _():
+            pl.semaphore_wait(come.at[2], 1)
+
+    sent = []
 
     def send(src, dst, s_sem, r_sem, to, cond=None):
         copy = pltpu.make_async_remote_copy(
@@ -104,7 +129,10 @@
     def g_unit(s, h, q):
         return g_all.at[at(s * 2 + h, half), at(place(q), ol)]
 
-    for h in (0, 1):
+    def far_first(depth):
+        return depth, 1 - depth
+
+    for h in far_first(d):
         to = 2 * d + h
         mine = to == r
         ours = g.at[at(d, half), at(h, ol)]
@@ -112,15 +140,19 @@
         send(theirs, g_unit(r, other, c), s_pre.at[h], g_z.at[r], {"depth": other}, mine)
         send(theirs, g_mid.at[h], s_pre.at[h], g_pre.at[h], {"depth": other}, jnp.logical_not(mine))
         local(ours, g_unit(r, d, c), g_z.at[r], mine)
-        send(ours, g_unit(r, d, c), s_z.at[h], g_z.at[r], {"row": to}, jnp.logical_not(mine))
+        near = jnp.logical_or(to == r + 1, to == r - 1)
+        send(ours, g_unit(r, d, c), s_z.at[h], g_z.at[r], {"row": to}, near)
+
+    def features(q, j):
+        return at(q * CHUNKS + j, ic)
 
     def send_tokens(j):
         for i, q in enumerate(peers):
             send(
-                tok.at[:, at(q * CHUNKS + j, ic)], x_all.at[j, at(r * 4 + c, tl)],
+                tok.at[:, features(q, j)], x_all.at[j, at(r * 4 + c, tl)],
                 s_xc.at[j, i], x_r.at[j, c], {"col": q},
             )
-        local(tok.at[:, at(c * CHUNKS + j, ic)], x_all.at[j, at(r * 4 + c, tl)], x_r.at[j, c])
+        local(tok.at[:, features(c, j)], x_all.at[j, at(r * 4 + c, tl)], x_r.at[j, c])
 
     def send_weight(j):
         for i, q in enumerate(peers):
@@ -134,11 +166,15 @@
         send_tokens(j)
     send_weight(0)
 
+    all_in()
+    for h in far_first(d):
+        to = 2 * d + h
+        away = jnp.logical_or(to > r + 1, to < r - 1)
+        send(g.at[at(d, half), at(h, ol)], g_unit(r, d, c), s_z.at[h], g_z.at[r], {"row": to}, away)
+
     def tokens_on(j, s, direction, cond):
         block = x_all.at[j, at(s, tb)]
         send(block, block, s_xz.at[j, direction, s], x_z.at[j, s], {"row": r + 1 - 2 * direction}, cond)
-
-    up_ok, down_ok = r < 3, r > 0
 
     def own_tokens_on(j):
         for q in range(4):
@@ -163,8 +199,14 @@
         s = order[n]
         unit = g_unit(s, d, c)
         arrived(unit, g_z.at[s])
+        send(unit, unit, s_y.at[0, s], g_y.at[0, s], {"depth": other})
+        if n < 3:
+            spread_across(n)
+
+    def spread_across(n):
+        s = order[n]
+        unit = g_unit(s, d, c)
         send(unit, unit, s_x.at[s], g_x.at[s], {"col": across})
-        send(unit, unit, s_y.at[0, s], g_y.at[0, s], {"depth": other})
 
     def crossed(n):
         s = order[n]
@@ -179,7 +221,8 @@
         slab = g_all.at[at(s, tb), at(k, 2 * ol)]
         send(slab, slab, s_d.at[s], g_d.at[s], {"col": core})
 
-    def pass_mid(h):
+    def pass_mid(i):
+        h = far_first(other)[i]
         to = 2 * other + h
         go = to != r
         arrived(g_mid.at[h], g_pre.at[h], go)
@@ -206,27 +249,32 @@
 
         lax.fori_loop(0, 4, body, None)
 
-    def multiply_weight(j):
+    def turn_tokens(j):
         def turn(b, carry):
             x_t[:, at(b, half)] = x_all[j, at(b, half), :].T
             return carry
 
         lax.fori_loop(0, 8, turn, None)
 
+    def multiply_columns(j, q_from, q_to):
+        gw_out[j, :, at(q_to, ol)] = jnp.dot(
+            x_t[...], g_all[:, at(q_from, ol)], preferred_element_type=F32
+        ).astype(BF16)
+
+    def multiply_weight(j):
+        turn_tokens(j)
+
         def body(n, carry):
-            cols = at(n, ol)
-            gw_out[j, :, cols] = jnp.dot(
-                x_t[...], g_all[:, cols], preferred_element_type=F32
-            ).astype(BF16)
+            multiply_columns(j, n, n)
             return carry
 
         lax.fori_loop(0, 4, body, None)
         for i, q in enumerate(peers):
             send(
-                gw_out.at[j, :, at(place(q), ol)], gw.at[at(c * CHUNKS + j, ic)],
+                gw_out.at[j, :, at(place(q), ol)], gw.at[features(c, j)],
                 s_gw.at[j, i], gw_r.at[j, c], {"col": q},
             )
-        local(gw_out.at[j, :, at(place(c), ol)], gw.at[at(c * CHUNKS + j, ic)], l_gw.at[j])
+        local(gw_out.at[j, :, at(place(c), ol)], gw.at[features(c, j)], l_gw.at[j])
 
     step = 64
     scale_rows = pl.ds(tb, GROUP)
@@ -330,9 +378,6 @@
             )
         local(gi_out.at[j, at(c, tl)], gi.at[:, at(c * CHUNKS + j, ic)], l_gi.at[j], cond)
 
-    inner = jnp.logical_or(r == 1, r == 2)
-    outer = jnp.logical_or(r == 0, r == 3)
-
     def run(name, f, *args):
         with jax.named_scope(name):
             f(*args)
@@ -360,66 +405,98 @@
     def ps(j, far):
         run("pass%d_%d" % (j, far), pass_tokens, j, far)
 
+    def l0(j, n):
+        run("l0_%d%d" % (j, n), level, j, 0, [n])
+
+    def l1(j, n):
+        run("l1_%d%d" % (j, n), level, j, 1, [n])
+
+    def l2(j, n):
+        run("l2_%d%d" % (j, n), level, j, 2, [n])
+
+    def l3(j):
+        run("l3_%d" % j, level, j, 3, [0])
+        end(j, outer, "out")
+
+    def some(j, n):
+        run("blk%d_%d" % (j, n), multiply_block, j, order[n])
+
     run("mid0", pass_mid, 0)
+    run("spread3", spread, 3)
     run("mid1", pass_mid, 1)
-    for j in range(CHUNKS):
-        run("own%d" % j, own_tokens_on, j)
-    run("spread3", spread, 3)
+    run("own0", own_tokens_on, 0)
+    run("own1", own_tokens_on, 1)
     for n in range(3):
         run("spread%d" % n, spread, n)
+    spread_across(3)
     for j in range(1, CHUNKS):
         send_weight(j)
+    run("own2", own_tokens_on, 2)
+    ps(0, 1)
+    run("own3", own_tokens_on, 3)
     run("crossed0", crossed, 0)
-    ps(0, 1)
     run("crossed1", crossed, 1)
-    run("to_core0", to_core, 0)
     ps(1, 1)
     run("crossed2", crossed, 2)
-    run("crossed3", crossed, 3)
+    ps(2, 1)
+    run("to_core0", to_core, 0)
     run("w_in0", weight_in, 0)
     block(0)
     run("to_core1", to_core, 1)
-    ps(2, 1)
+    run("crossed3", crossed, 3)
+    ps(0, 2)
     block(1)
+    ps(3, 1)
     run("to_core2", to_core, 2)
-    ps(3, 1)
     block(2)
+    l1(0, 0)
     run("to_core3", to_core, 3)
-    ps(0, 2)
+    ps(1, 2)
+    run("w_in1", weight_in, 1)
+    for n in range(3):
+        some(1, n)
+        l0(1, n)
     block(3)
-    ps(1, 2)
-    mi(1)
-    lv(1, 0)
+    some(1, 3)
+    l1(0, 1)
+    l1(0, 2)
     ps(2, 2)
-    lv(0, 1)
     mw(0)
     mi(2)
-    lv(2, 0)
+    for n in range(3):
+        l0(2, n)
+    l1(1, 0)
+    l2(0, 0)
+    l1(1, 1)
+    l2(0, 1)
+    end(0, inner, "in")
+    l1(1, 2)
     ps(3, 2)
-    lv(0, 2)
-    end(0, inner, "in")
-    lv(1, 1)
+    mw(1)
     mi(3)
-    lv(3, 0)
-    mw(1)
-    lv(0, 3)
-    end(0, outer, "out")
-    lv(1, 2)
+    for n in range(3):
+        l0(3, n)
+    l3(0)
+    l2(1, 0)
+    l1(2, 0)
+    l2(1, 1)
     end(1, inner, "in")
     mw(2)
-    lv(2, 1)
-    lv(1, 3)
-    end(1, outer, "out")
-    lv(2, 2)
+    l1(2, 1)
+    l3(1)
+    l1(2, 2)
+    l2(2, 0)
+    l2(2, 1)
     end(2, inner, "in")
     mw(3)
-    lv(3, 1)
-    lv(2, 3)
-    end(2, outer, "out")
-    lv(3, 2)
+    l1(3, 0)
+    l3(2)
+    l1(3, 1)
+    l1(3, 2)
+    l2(3, 0)
+    l2(3, 1)
     end(3, inner, "in")
-    lv(3, 3)
-    end(3, outer, "out")
+    l3(3)
 
     def drain():
         for wait, cond in sent:
@@ -427,11 +504,11 @@
 
     def outputs():
         for j in range(CHUNKS):
-            arrived(gi.at[:, at(c * CHUNKS + j, ic)], l_gi.at[j])
-            arrived(gw.at[at(c * CHUNKS + j, ic)], l_gw.at[j])
+            arrived(gi.at[:, features(c, j)], l_gi.at[j])
+            arrived(gw.at[features(c, j)], l_gw.at[j])
             for q in peers:
-                arrived(gi.at[:, at(q * CHUNKS + j, ic)], gi_r.at[j, q])
-                arrived(gw.at[at(q * CHUNKS + j, ic)], gw_r.at[j, q])
+                arrived(gi.at[:, features(q, j)], gi_r.at[j, q])
+                arrived(gw.at[features(q, j)], gw_r.at[j, q])
 
     run("drain", drain)
     run("outputs", outputs)
@@ -468,7 +545,7 @@
             dma((2,)), dma((4,)), dma((4,)), dma((2, 4)), dma((4,)),
             dma((CHUNKS, 3)), dma((CHUNKS, 3)), dma((CHUNKS, 2, 4)),
             dma((3 * CHUNKS,)), dma((3 * CHUNKS,)), dma((CHUNKS, 3)), dma((CHUNKS, 3)),
-            dma((CHUNKS,)), dma((CHUNKS,)),
+            dma((CHUNKS,)), dma((CHUNKS,)), pltpu.SemaphoreType.REGULAR((3,)),
         ],
         compiler_params=pltpu.CompilerParams(
             collective_id=0, has_side_effects=True, vmem_limit_bytes=46 * 2**20

time: 150 us -> 146 us (0.973); the launches traced: 150 us -> 145 us
  Pallas kernels: 147 us -> 141 us
    pallas_call x1, Pallas kernels: 147 us -> 141 us  [per_device_kernel(): pl.pallas_call(kernel, out_shape=(jax.ShapeDtypeStruct(tokens.shape, BF16...]
where the time goes in v3:
time: 146 us; the launch traced here: 145 us
  Pallas kernels  141 us (97%)
  local copies, waits for them, and re-layouts  2.99 us (2%)
    pallas_call x1, Pallas kernels, per_device_kernel(): pl.pallas_call(kernel, out_shape=(jax.ShapeDtypeStruct(tokens.shape, BF16...  141 us
    unnamed x2, local copies, waits for them, and re-layouts  2.99 us

profile of v3, /device:TPU:21, one launch (start us, length us, event | category | flops | bytes accessed | tf_op | source)
XLA Modules:
  0.0 144.6 jit_solution(10628267256625096162)
XLA Ops:
  0.6 140.9 %shard_map.50 = (bf16[128,4096]{1,0:T(8,128)(2,1)S(1)}, bf16[4096,512]{1,0:T(8,128)(2,1)S(1)}) custom-call(bf16[128,4096]{1,0:T(8,128)(2,1)} %tok.1, bf16[4096,512]{1,0:T(8,128)(2,1)} %w.1, bf16[512,1024]{1,0:T(8,128)(2,1)} %g.1), custom_call_target="tpu_custom_call" | custom-call | tf_op jit(solution)/shard_map/pallas_call | solution.py:524
  141.6 1.0 copy.7
  142.5 2.0 %copy.8 = bf16[4096,512]{1,0:T(8,128)(2,1)} copy(bf16[4096,512]{1,0:T(8,128)(2,1)S(1)} %get-tuple-element.5) | data formatting | bytes 8388608

commit v4 on v3

--- a/solution.py
+++ b/solution.py
@@ -8,7 +8,9 @@
 last_with_last = (((1,), (1,)), ((), ()))
 first_with_first = (((0,), (0,)), ((), ()))
 MESH = pl.DeviceIdType.MESH
+PRE, Z, X, Y, CORE, TOK, HOME, W, UP, DOWN, TOK_UP, TOK_DOWN, HOME_UP, HOME_DOWN, GI, GW = range(16)
 CHUNKS = 4
+LAST = CHUNKS - 1
 GROUP = 16
 SPAN = 83.0
 TINY = 1e-30
@@ -52,8 +54,7 @@
 def kernel(
     tok, w, g, gi, gw,
     g_all, g_mid, x_all, x_t, w_all, part, gw_out, gi_out, ups, upr, dns, dnr,
-    g_pre, g_z, g_x, g_y, g_d, x_r, w_r, x_z, up_r, dn_r, gi_r, gw_r,
-    s_pre, s_z, s_x, s_y, s_d, s_xc, s_w, s_xz, s_up, s_dn, s_gi, s_gw, l_gi, l_gw, come,
+    x_home, come, g_pre, g_z, g_x, g_y, g_d, x_r, w_r, x_z, up_r, dn_r, done, gone,
 ):
     r, c, d = lax.axis_index("row"), lax.axis_index("col"), lax.axis_index("depth")
     k, x = c % 2, c // 2
@@ -108,14 +109,11 @@
         def _():
             pl.semaphore_wait(come.at[2], 1)
 
-    sent = []
-
-    def send(src, dst, s_sem, r_sem, to, cond=None):
+    def send(src, dst, kind, r_sem, to, cond=None):
         copy = pltpu.make_async_remote_copy(
-            src_ref=src, dst_ref=dst, send_sem=s_sem, recv_sem=r_sem, device_id=to, device_id_type=MESH
+            src_ref=src, dst_ref=dst, send_sem=gone.at[kind], recv_sem=r_sem, device_id=to, device_id_type=MESH
         )
         when(cond, copy.start)
-        sent.append((copy.wait_send, cond))
 
     def local(src, dst, sem, cond=None):
         when(cond, pltpu.make_async_copy(src, dst, sem).start)
@@ -137,11 +135,11 @@
         mine = to == r
         ours = g.at[at(d, half), at(h, ol)]
         theirs = g.at[at(other, half), at(h, ol)]
-        send(theirs, g_unit(r, other, c), s_pre.at[h], g_z.at[r], {"depth": other}, mine)
-        send(theirs, g_mid.at[h], s_pre.at[h], g_pre.at[h], {"depth": other}, jnp.logical_not(mine))
+        send(theirs, g_unit(r, other, c), PRE, g_z.at[r], {"depth": other}, mine)
+        send(theirs, g_mid.at[h], PRE, g_pre.at[h], {"depth": other}, jnp.logical_not(mine))
         local(ours, g_unit(r, d, c), g_z.at[r], mine)
         near = jnp.logical_or(to == r + 1, to == r - 1)
-        send(ours, g_unit(r, d, c), s_z.at[h], g_z.at[r], {"row": to}, near)
+        send(ours, g_unit(r, d, c), Z, g_z.at[r], {"row": to}, near)
 
     def features(q, j):
         return at(q * CHUNKS + j, ic)
@@ -150,35 +148,51 @@
         for i, q in enumerate(peers):
             send(
                 tok.at[:, features(q, j)], x_all.at[j, at(r * 4 + c, tl)],
-                s_xc.at[j, i], x_r.at[j, c], {"col": q},
+                TOK, x_r.at[j], {"col": q},
             )
-        local(tok.at[:, features(c, j)], x_all.at[j, at(r * 4 + c, tl)], x_r.at[j, c])
+        local(tok.at[:, features(c, j)], x_all.at[j, at(r * 4 + c, tl)], x_r.at[j])
+
+    def home(q):
+        return at((q * CHUNKS + LAST) * 2 + 1, ic // 2)
+
+    def facing(q):
+        return q + 2 - 4 * (q // 2)
+
+    def send_home_tokens():
+        rows = at(r * 4 + c, tl)
+        for i, q in enumerate(peers):
+            send(tok.at[:, home(facing(q))], x_home.at[rows], HOME, x_r.at[CHUNKS], {"col": q})
+        local(tok.at[:, home(across)], x_home.at[rows], x_r.at[CHUNKS])
 
     def send_weight(j):
         for i, q in enumerate(peers):
             send(
                 w.at[at(q * CHUNKS + j, ic)], w_all.at[j, :, at(place(c), ol)],
-                s_w.at[j, i], w_r.at[j, c], {"col": q},
+                W, w_r.at[j], {"col": q},
             )
-        local(w.at[at(c * CHUNKS + j, ic)], w_all.at[j, :, at(place(c), ol)], w_r.at[j, c])
+        local(w.at[at(c * CHUNKS + j, ic)], w_all.at[j, :, at(place(c), ol)], w_r.at[j])
 
     for j in range(CHUNKS):
         send_tokens(j)
+    send_home_tokens()
     send_weight(0)
 
     all_in()
     for h in far_first(d):
         to = 2 * d + h
         away = jnp.logical_or(to > r + 1, to < r - 1)
-        send(g.at[at(d, half), at(h, ol)], g_unit(r, d, c), s_z.at[h], g_z.at[r], {"row": to}, away)
+        send(g.at[at(d, half), at(h, ol)], g_unit(r, d, c), Z, g_z.at[r], {"row": to}, away)
+
+    def gathered(j, s, n):
+        return x_all.at[j, at(s, n)] if j < CHUNKS else x_home.at[at(s, n)]
 
     def tokens_on(j, s, direction, cond):
-        block = x_all.at[j, at(s, tb)]
-        send(block, block, s_xz.at[j, direction, s], x_z.at[j, s], {"row": r + 1 - 2 * direction}, cond)
+        block = gathered(j, s, tb)
+        kind = (TOK_UP if j < CHUNKS else HOME_UP) + direction
+        send(block, block, kind, x_z.at[j, s], {"row": r + 1 - 2 * direction}, cond)
 
     def own_tokens_on(j):
-        for q in range(4):
-            arrived(x_all.at[j, at(r * 4 + q, tl)], x_r.at[j, q])
+        arrived(gathered(j, r, tb), x_r.at[j])
         tokens_on(j, r, 0, up_ok)
         tokens_on(j, r, 1, down_ok)
 
@@ -186,9 +200,9 @@
         below, above = r - far, r + far
         low, high = jnp.maximum(below, 0), jnp.minimum(above, 3)
         has_low, has_high = below >= 0, above <= 3
-        arrived(x_all.at[j, at(low, tb)], x_z.at[j, low], has_low)
+        arrived(gathered(j, low, tb), x_z.at[j, low], has_low)
         tokens_on(j, low, 0, jnp.logical_and(has_low, up_ok))
-        arrived(x_all.at[j, at(high, tb)], x_z.at[j, high], has_high)
+        arrived(gathered(j, high, tb), x_z.at[j, high], has_high)
         tokens_on(j, high, 1, jnp.logical_and(has_high, down_ok))
 
     near = 3 * (1 - r // 2)
@@ -199,42 +213,40 @@
         s = order[n]
         unit = g_unit(s, d, c)
         arrived(unit, g_z.at[s])
-        send(unit, unit, s_y.at[0, s], g_y.at[0, s], {"depth": other})
+        send(unit, unit, Y, g_y.at[s], {"depth": other})
         if n < 3:
             spread_across(n)
 
     def spread_across(n):
         s = order[n]
         unit = g_unit(s, d, c)
-        send(unit, unit, s_x.at[s], g_x.at[s], {"col": across})
+        send(unit, unit, X, g_x.at[s], {"col": across})
 
     def crossed(n):
         s = order[n]
         unit = g_unit(s, d, across)
         arrived(unit, g_x.at[s])
-        send(unit, unit, s_y.at[1, s], g_y.at[1, s], {"depth": other})
+        send(unit, unit, Y, g_y.at[s], {"depth": other})
 
     def to_core(n):
         s = order[n]
-        arrived(g_unit(s, other, c), g_y.at[0, s])
-        arrived(g_unit(s, other, across), g_y.at[1, s])
+        arrived(g_all.at[at(s * 2 + other, half), at(k, 2 * ol)], g_y.at[s])
         slab = g_all.at[at(s, tb), at(k, 2 * ol)]
-        send(slab, slab, s_d.at[s], g_d.at[s], {"col": core})
+        send(slab, slab, CORE, g_d.at[s], {"col": core})
 
     def pass_mid(i):
         h = far_first(other)[i]
         to = 2 * other + h
         go = to != r
         arrived(g_mid.at[h], g_pre.at[h], go)
-        send(g_mid.at[h], g_unit(r, d, c), s_z.at[2 + h], g_z.at[r], {"row": to}, go)
+        send(g_mid.at[h], g_unit(r, d, c), Z, g_z.at[r], {"row": to}, go)
 
     def from_core(n):
         s = order[n]
         arrived(g_all.at[at(s, tb), at(1 - k, 2 * ol)], g_d.at[s])
 
     def weight_in(j):
-        for q in range(4):
-            arrived(w_all.at[j, :, at(place(q), ol)], w_r.at[j, q])
+        arrived(w_all.at[j], w_r.at[j])
 
     def multiply_block(j, s):
         rows = at(s, tb)
@@ -256,25 +268,75 @@
 
         lax.fori_loop(0, 8, turn, None)
 
-    def multiply_columns(j, q_from, q_to):
-        gw_out[j, :, at(q_to, ol)] = jnp.dot(
-            x_t[...], g_all[:, at(q_from, ol)], preferred_element_type=F32
-        ).astype(BF16)
+    def multiply_columns(rows, q):
+        return jnp.dot(x_t[rows, :], g_all[:, at(q, ol)], preferred_element_type=F32).astype(BF16)
 
     def multiply_weight(j):
         turn_tokens(j)
 
         def body(n, carry):
-            multiply_columns(j, n, n)
+            gw_out[j, :, at(n, ol)] = multiply_columns(pl.ds(0, ic), n)
             return carry
 
         lax.fori_loop(0, 4, body, None)
         for i, q in enumerate(peers):
             send(
                 gw_out.at[j, :, at(place(q), ol)], gw.at[features(c, j)],
-                s_gw.at[j, i], gw_r.at[j, c], {"col": q},
+                GW, done.at[1], {"col": q},
             )
-        local(gw_out.at[j, :, at(place(c), ol)], gw.at[features(c, j)], l_gw.at[j])
+        local(gw_out.at[j, :, at(place(c), ol)], gw.at[features(c, j)], done.at[1])
+
+    first, second = pl.ds(0, ic // 2), pl.ds(ic // 2, ic // 2)
+
+    def front(q):
+        return at((q * CHUNKS + LAST) * 2, ic // 2)
+
+    def multiply_weight_last():
+        turn_tokens(LAST)
+
+        def body(n, carry):
+            q = 2 * n + 1 - x
+            gw_out[LAST, first, at(q, ol)] = multiply_columns(first, q)
+            return carry
+
+        lax.fori_loop(0, 2, body, None)
+        for i, q in enumerate((across, diagonal)):
+            send(
+                gw_out.at[LAST, first, at(place(q), ol)], gw.at[front(c)],
+                GW, done.at[1], {"col": q},
+            )
+
+        def body(n, carry):
+            q = 2 * n + x
+            gw_out[LAST, :, at(q, ol)] = multiply_columns(pl.ds(0, ic), q)
+            return carry
+
+        lax.fori_loop(0, 2, body, None)
+        rows = features(c, LAST)
+        send(
+            gw_out.at[LAST, :, at(place(core), ol)], gw.at[rows],
+            GW, done.at[1], {"col": core},
+        )
+        local(gw_out.at[LAST, :, at(place(c), ol)], gw.at[rows], done.at[1])
+
+    def multiply_weight_home():
+        def turn(b, carry):
+            x_t[first, at(b, half)] = x_home[at(b, half), :].T
+            return carry
+
+        lax.fori_loop(0, 8, turn, None)
+
+        def body(n, carry):
+            gw_out[LAST, second, at(2 * n + 1 - x, ol)] = multiply_columns(first, 2 * n + x)
+            return carry
+
+        lax.fori_loop(0, 2, body, None)
+        rows = home(across)
+        send(
+            gw_out.at[LAST, second, at(place(diagonal), ol)], gw.at[rows],
+            GW, done.at[1], {"col": core},
+        )
+        local(gw_out.at[LAST, second, at(place(across), ol)], gw.at[rows], done.at[1])
 
     step = 64
     scale_rows = pl.ds(tb, GROUP)
@@ -332,7 +394,7 @@
 
     def ring(j, level, up, which):
         here = level if up else 3 - level
-        out, got, s_sem, r_sem = (ups, upr, s_up, up_r) if up else (dns, dnr, s_dn, dn_r)
+        out, got, kind, r_sem = (ups, upr, UP, up_r) if up else (dns, dnr, DOWN, dn_r)
         toward = {"row": r + 1 if up else r - 1}
         far = [3, 2, 1, 0] if up else [0, 1, 2, 3]
         cond = r == here
@@ -348,7 +410,7 @@
 
                 continue
             copy = pltpu.make_async_remote_copy(
-                src_ref=out.at[i], dst_ref=got.at[i], send_sem=s_sem.at[i], recv_sem=r_sem.at[i],
+                src_ref=out.at[i], dst_ref=got.at[i], send_sem=gone.at[kind], recv_sem=r_sem.at[i],
                 device_id=toward, device_id_type=MESH,
             )
 
@@ -359,8 +421,6 @@
                 encode(j, b, out, i, got if level > 0 else None)
                 copy.start()
 
-            sent.append((copy.wait_send, cond))
-
     def level(j, n, which=None):
         which = range(4 - n if n else 3) if which is None else which
         ring(j, n, True, which)
@@ -374,9 +434,9 @@
         for i, q in enumerate(peers):
             send(
                 gi_out.at[j, at(q, tl)], gi.at[:, at(c * CHUNKS + j, ic)],
-                s_gi.at[j, i], gi_r.at[j, c], {"col": q}, cond,
+                GI, done.at[0], {"col": q}, cond,
             )
-        local(gi_out.at[j, at(c, tl)], gi.at[:, at(c * CHUNKS + j, ic)], l_gi.at[j], cond)
+        local(gi_out.at[j, at(c, tl)], gi.at[:, at(c * CHUNKS + j, ic)], done.at[0], cond)
 
     def run(name, f, *args):
         with jax.named_scope(name):
@@ -388,7 +448,7 @@
 
     def mw(j):
         run("pass%d_3" % j, pass_tokens, j, 3)
-        run("weight%d" % j, multiply_weight, j)
+        run("weight%d" % j, multiply_weight if j < LAST else multiply_weight_last, *([j] if j < LAST else []))
 
     def lv(j, n, which=None):
         run("level%d_%d" % (j, n), level, j, n, which)
@@ -421,10 +481,10 @@
     def some(j, n):
         run("blk%d_%d" % (j, n), multiply_block, j, order[n])
 
+    run("own0", own_tokens_on, 0)
     run("mid0", pass_mid, 0)
     run("spread3", spread, 3)
     run("mid1", pass_mid, 1)
-    run("own0", own_tokens_on, 0)
     run("own1", own_tokens_on, 1)
     for n in range(3):
         run("spread%d" % n, spread, n)
@@ -434,6 +494,7 @@
     run("own2", own_tokens_on, 2)
     ps(0, 1)
     run("own3", own_tokens_on, 3)
+    run("own4", own_tokens_on, 4)
     run("crossed0", crossed, 0)
     run("crossed1", crossed, 1)
     ps(1, 1)
@@ -447,6 +508,7 @@
     ps(0, 2)
     block(1)
     ps(3, 1)
+    ps(4, 1)
     run("to_core2", to_core, 2)
     block(2)
     l1(0, 0)
@@ -472,6 +534,7 @@
     end(0, inner, "in")
     l1(1, 2)
     ps(3, 2)
+    ps(4, 2)
     mw(1)
     mi(3)
     for n in range(3):
@@ -483,35 +546,81 @@
     end(1, inner, "in")
     mw(2)
     l1(2, 1)
+    l2(2, 0)
     l3(1)
     l1(2, 2)
-    l2(2, 0)
+    mw(3)
+    l1(3, 0)
     l2(2, 1)
     end(2, inner, "in")
-    mw(3)
-    l1(3, 0)
     l3(2)
     l1(3, 1)
+    l2(3, 0)
     l1(3, 2)
-    l2(3, 0)
     l2(3, 1)
     end(3, inner, "in")
+    ps(4, 3)
+    run("home", multiply_weight_home)
     l3(3)
 
     def drain():
-        for wait, cond in sent:
-            when(cond, wait)
+        def all_gone(kind, ref, cond=None):
+            arrived(ref, gone.at[kind], cond)
+
+        def units(n):
+            return g_all.at[pl.ds(0, n * half // 4)]
+
+        for kind, n in ((PRE, 2), (Z, 3), (X, 4), (Y, 8), (CORE, 16)):
+            all_gone(kind, units(n))
+        all_gone(TOK, x_all.at[0, pl.ds(0, 3 * CHUNKS * tl)])
+        all_gone(HOME, x_home.at[pl.ds(0, 3 * tl)])
+        all_gone(W, w_all.at[pl.ds(0, 3)])
+        for n in range(3):
+            for at_n, tok_kind, home_kind, kind, ref in (
+                (r == n, TOK_UP, HOME_UP, UP, ups), (r == 3 - n, TOK_DOWN, HOME_DOWN, DOWN, dns)
+            ):
+                all_gone(tok_kind, x_all.at[pl.ds(0, n + 1)], at_n)
+                all_gone(home_kind, x_home.at[pl.ds(0, (n + 1) * tb)], at_n)
+                all_gone(kind, ref.at[pl.ds(0, (3 - n) * CHUNKS)], at_n)
+        all_gone(GI, x_all.at[0, pl.ds(0, 3 * CHUNKS * tl)])
+        all_gone(GW, g_all.at[pl.ds(0, (6 * LAST + 5) * ic // 8)])
 
     def outputs():
-        for j in range(CHUNKS):
-            arrived(gi.at[:, features(c, j)], l_gi.at[j])
-            arrived(gw.at[features(c, j)], l_gw.at[j])
-            for q in peers:
-                arrived(gi.at[:, features(q, j)], gi_r.at[j, q])
-                arrived(gw.at[features(q, j)], gw_r.at[j, q])
+        arrived(gi, done.at[0])
+        arrived(gw, done.at[1])
 
     run("drain", drain)
     run("outputs", outputs)
+
+
+PIECES = 4
+
+
+def store_kernel(gi_in, gw_in, gi, gw, sem):
+    n = gw.shape[0] // PIECES
+    copies = [
+        pltpu.make_async_copy(gw_in.at[pl.ds(i * n, n)], gw.at[pl.ds(i * n, n)], sem.at[i])
+        for i in range(PIECES)
+    ] + [pltpu.make_async_copy(gi_in, gi, sem.at[PIECES])]
+    for copy in copies:
+        copy.start()
+    for copy in copies:
+        copy.wait()
+
+
+def store(grad_input, grad_weight):
+    anywhere = pl.BlockSpec(memory_space=pl.ANY)
+    return pl.pallas_call(
+        store_kernel,
+        out_shape=(
+            jax.ShapeDtypeStruct(grad_input.shape, BF16),
+            jax.ShapeDtypeStruct(grad_weight.shape, BF16),
+        ),
+        in_specs=[anywhere] * 2,
+        out_specs=(anywhere, anywhere),
+        scratch_shapes=[pltpu.SemaphoreType.DMA((PIECES + 1,))],
+        compiler_params=pltpu.CompilerParams(vmem_limit_bytes=2**20),
+    )(grad_input, grad_weight)
 
 
 def per_device_kernel(tokens, weight, grad_output):
@@ -521,7 +630,7 @@
     dma = pltpu.SemaphoreType.DMA
     code = pltpu.VMEM((3 * CHUNKS, tb + GROUP, ic), BF16)
     anywhere = pl.BlockSpec(memory_space=pl.ANY)
-    return pl.pallas_call(
+    return store(*pl.pallas_call(
         kernel,
         out_shape=(
             jax.ShapeDtypeStruct(tokens.shape, BF16),
@@ -539,18 +648,14 @@
             pltpu.VMEM((CHUNKS, ic, 4 * ol), BF16),
             pltpu.VMEM((CHUNKS, tb, ic), BF16),
             code, code, code, code,
-            dma((2,)), dma((4,)), dma((4,)), dma((2, 4)), dma((4,)),
-            dma((CHUNKS, 4)), dma((CHUNKS, 4)), dma((CHUNKS, 4)),
-            dma((3 * CHUNKS,)), dma((3 * CHUNKS,)), dma((CHUNKS, 4)), dma((CHUNKS, 4)),
-            dma((2,)), dma((4,)), dma((4,)), dma((2, 4)), dma((4,)),
-            dma((CHUNKS, 3)), dma((CHUNKS, 3)), dma((CHUNKS, 2, 4)),
-            dma((3 * CHUNKS,)), dma((3 * CHUNKS,)), dma((CHUNKS, 3)), dma((CHUNKS, 3)),
-            dma((CHUNKS,)), dma((CHUNKS,)), pltpu.SemaphoreType.REGULAR((3,)),
+            pltpu.VMEM((4 * tb, ic // 2), BF16), pltpu.SemaphoreType.REGULAR((3,)),
+            dma((2,)), dma((4,)), dma((4,)), dma((4,)), dma((4,)), dma((CHUNKS + 1,)), dma((CHUNKS,)),
+            dma((CHUNKS + 1, 4)), dma((3 * CHUNKS,)), dma((3 * CHUNKS,)), dma((2,)), dma((16,)),
         ],
         compiler_params=pltpu.CompilerParams(
             collective_id=0, has_side_effects=True, vmem_limit_bytes=46 * 2**20
         ),
-    )(*[pltpu.with_memory_space_constraint(a, pltpu.HBM) for a in (tokens, weight, grad_output)])
+    )(*[pltpu.with_memory_space_constraint(a, pltpu.HBM) for a in (tokens, weight, grad_output)]))
 
 
 def solution(mesh):

time: 146 us -> 142 us (0.973)
  the two profiles are of different devices: /device:TPU:21 before, /device:TPU:0 now
where the time goes in v4:
time: 142 us
  Pallas kernels  141 us (99%)
    pallas_call x1, Pallas kernels, per_device_kernel(): pl.pallas_call(kernel, out_shape=(jax.ShapeDtypeStruct(tokens.shape, BF16...  139 us

profile of v4, /device:TPU:0, one launch (start us, length us, event | category | flops | bytes accessed | tf_op | source)
XLA Modules:
  0.0 141.9 jit_solution(14695466628968793286)
XLA Ops:
  0.6 138.7 %shard_map.50 = (bf16[128,4096]{1,0:T(8,128)(2,1)S(1)}, bf16[4096,512]{1,0:T(8,128)(2,1)S(1)}) custom-call(bf16[128,4096]{1,0:T(8,128)(2,1)} %tok.1, bf16[4096,512]{1,0:T(8,128)(2,1)} %w.1, bf16[512,1024]{1,0:T(8,128)(2,1)} %g.1), custom_call_target="tpu_custom_call" | custom-call | tf_op jit(solution)/shard_map/pallas_call | solution.py:633
  139.4 2.4 %shard_map.51 = (bf16[128,4096]{1,0:T(8,128)(2,1)}, bf16[4096,512]{1,0:T(8,128)(2,1)}) custom-call(bf16[128,4096]{1,0:T(8,128)(2,1)S(1)} %get-tuple-element.4.gi_in, bf16[4096,512]{1,0:T(8,128)(2,1)S(1)} %get-tuple-element.5.gw_in), custom_call_target="tpu_custom_call" | custom-call | tf_op jit(solution)/shard_map/pallas_call | solution.py:613

commit v5 on v4

--- a/solution.py
+++ b/solution.py
@@ -8,7 +8,7 @@
 last_with_last = (((1,), (1,)), ((), ()))
 first_with_first = (((0,), (0,)), ((), ()))
 MESH = pl.DeviceIdType.MESH
-PRE, Z, X, Y, CORE, TOK, HOME, W, UP, DOWN, TOK_UP, TOK_DOWN, HOME_UP, HOME_DOWN, GI, GW = range(16)
+PRE, Z, X, Y, CORE, TOK, HOME, W, UP, DOWN, TOK_UP, TOK_DOWN, HOME_UP, HOME_DOWN, UP2, DOWN2, GI, GW = range(18)
 CHUNKS = 4
 LAST = CHUNKS - 1
 GROUP = 16
@@ -53,7 +53,7 @@
 
 def kernel(
     tok, w, g, gi, gw,
-    g_all, g_mid, x_all, x_t, w_all, part, gw_out, gi_out, ups, upr, dns, dnr,
+    g_all, g_mid, x_all, x_t, w_all, part, gw_out, gi_out, ups, upr, dns, dnr, ups2, upr2, dns2, dnr2,
     x_home, come, g_pre, g_z, g_x, g_y, g_d, x_r, w_r, x_z, up_r, dn_r, done, gone,
 ):
     r, c, d = lax.axis_index("row"), lax.axis_index("col"), lax.axis_index("depth")
@@ -339,6 +339,19 @@
         local(gw_out.at[LAST, second, at(place(across), ol)], gw.at[rows], done.at[1])
 
     step = 64
+
+    def chunk_of(p):
+        return min(p, LAST)
+
+    def columns_of(p):
+        return pl.ds(0, ic) if p < LAST else at(p - LAST, ic // 2)
+
+    def features_of(p):
+        return at(c * CHUNKS + p, ic) if p < LAST else at((c * CHUNKS + LAST) * 2 + p - LAST, ic // 2)
+
+    def part_at(p, b, t):
+        return chunk_of(p), pl.ds(pl.multiple_of(b * tb + t * step, step), step), columns_of(p)
+
     scale_rows = pl.ds(tb, GROUP)
 
     def read_code(buf, i, rows, unit):
@@ -350,11 +363,11 @@
     def unit_of(buf, i):
         return buf[i, scale_rows, :].astype(F32) * (0.5 / SPAN)
 
-    def encode(j, b, out, slot, got):
+    def encode(p, b, out, slot, got):
         unit = None if got is None else unit_of(got, slot)
 
         def total(t):
-            value = part[j, pl.ds(pl.multiple_of(b * tb + t * step, step), step), :]
+            value = part[part_at(p, b, t)]
             if got is not None:
                 value = value + read_code(got, slot, at(t, step), unit)
             return value
@@ -362,81 +375,87 @@
         def first(t, most):
             value = total(t)
             if got is not None:
-                part[j, pl.ds(pl.multiple_of(b * tb + t * step, step), step), :] = value
+                part[part_at(p, b, t)] = value
             size = jnp.abs(value)
             for n in range(step // GROUP):
                 most = jnp.maximum(most, size[n * GROUP : (n + 1) * GROUP])
             return most
 
-        most = lax.fori_loop(0, tb // step, first, jnp.full((GROUP, ic), TINY, F32))
+        most = lax.fori_loop(0, tb // step, first, jnp.full((GROUP, out.shape[-1]), TINY, F32))
         scale = (most * 1.01).astype(BF16)
         out[slot, scale_rows, :] = scale
         by = (2 * SPAN) / scale.astype(F32)
         by = jnp.concatenate([by] * (step // GROUP), axis=0)
 
         def second(t, carry):
-            value = part[j, pl.ds(pl.multiple_of(b * tb + t * step, step), step), :]
+            value = part[part_at(p, b, t)]
             code = jnp.exp(jnp.abs(value) * by - SPAN)
             out[slot, at(t, step), :] = jnp.where(value < 0, -code, code).astype(BF16)
             return carry
 
         lax.fori_loop(0, tb // step, second, None)
 
-    def add_in(j, got, slot):
+    def add_in(p, got, slot):
         unit = unit_of(got, slot)
 
         def body(t, carry):
-            rows = pl.ds(pl.multiple_of(r * tb + t * step, step), step)
-            part[j, rows, :] = part[j, rows, :] + read_code(got, slot, at(t, step), unit)
+            where = part_at(p, r, t)
+            part[where] = part[where] + read_code(got, slot, at(t, step), unit)
             return carry
 
         lax.fori_loop(0, tb // step, body, None)
 
-    def ring(j, level, up, which):
+    def ring(p, level, up, which):
         here = level if up else 3 - level
-        out, got, kind, r_sem = (ups, upr, UP, up_r) if up else (dns, dnr, DOWN, dn_r)
+        if p < LAST:
+            out, got, kind, r_sem = (ups, upr, UP, up_r) if up else (dns, dnr, DOWN, dn_r)
+        else:
+            out, got, kind, r_sem = (ups2, upr2, UP2, up_r) if up else (dns2, dnr2, DOWN2, dn_r)
         toward = {"row": r + 1 if up else r - 1}
         far = [3, 2, 1, 0] if up else [0, 1, 2, 3]
         cond = r == here
         for n in which:
             b = far[n]
-            i = j * 3 + (b - 1 if up else b)
+            m = p * 3 + (b - 1 if up else b)
+            i = m if p < LAST else m - 3 * LAST
             if b == here:
 
                 @pl.when(cond)
                 def _():
-                    arrived(got.at[i], r_sem.at[i])
-                    add_in(j, got, i)
+                    arrived(got.at[i], r_sem.at[m])
+                    add_in(p, got, i)
 
                 continue
             copy = pltpu.make_async_remote_copy(
-                src_ref=out.at[i], dst_ref=got.at[i], send_sem=gone.at[kind], recv_sem=r_sem.at[i],
+                src_ref=out.at[i], dst_ref=got.at[i], send_sem=gone.at[kind], recv_sem=r_sem.at[m],
                 device_id=toward, device_id_type=MESH,
             )
 
             @pl.when(cond)
             def _():
                 if level > 0:
-                    arrived(got.at[i], r_sem.at[i])
-                encode(j, b, out, i, got if level > 0 else None)
+                    arrived(got.at[i], r_sem.at[m])
+                encode(p, b, out, i, got if level > 0 else None)
                 copy.start()
 
-    def level(j, n, which=None):
+    def level(p, n, which=None):
         which = range(4 - n if n else 3) if which is None else which
-        ring(j, n, True, which)
-        ring(j, n, False, which)
-
-    def finish(j, cond):
+        ring(p, n, True, which)
+        ring(p, n, False, which)
+
+    def finish(p, cond):
+        j, columns = chunk_of(p), columns_of(p)
+
         @pl.when(cond)
         def _():
-            gi_out[j] = part[j, at(r, tb), :].astype(BF16)
-
-        for i, q in enumerate(peers):
+            gi_out[j, :, columns] = part[j, at(r, tb), columns].astype(BF16)
+
+        for q in peers:
             send(
-                gi_out.at[j, at(q, tl)], gi.at[:, at(c * CHUNKS + j, ic)],
+                gi_out.at[j, at(q, tl), columns], gi.at[:, features_of(p)],
                 GI, done.at[0], {"col": q}, cond,
             )
-        local(gi_out.at[j, at(c, tl)], gi.at[:, at(c * CHUNKS + j, ic)], done.at[0], cond)
+        local(gi_out.at[j, at(c, tl), columns], gi.at[:, features_of(p)], done.at[0], cond)
 
     def run(name, f, *args):
         with jax.named_scope(name):
@@ -537,8 +556,9 @@
     ps(4, 2)
     mw(1)
     mi(3)
-    for n in range(3):
-        l0(3, n)
+    for p in (LAST, LAST + 1):
+        for n in range(3):
+            l0(p, n)
     l3(0)
     l2(1, 0)
     l1(2, 0)
@@ -557,11 +577,19 @@
     l1(3, 1)
     l2(3, 0)
     l1(3, 2)
+    l1(4, 0)
     l2(3, 1)
     end(3, inner, "in")
+    l1(4, 1)
+    l3(3)
+    l2(4, 0)
+    l1(4, 2)
+    l2(4, 1)
+    end(4, inner, "in")
     ps(4, 3)
     run("home", multiply_weight_home)
-    l3(3)
+    l3(4)
+
 
     def drain():
         def all_gone(kind, ref, cond=None):
@@ -576,12 +604,14 @@
         all_gone(HOME, x_home.at[pl.ds(0, 3 * tl)])
         all_gone(W, w_all.at[pl.ds(0, 3)])
         for n in range(3):
-            for at_n, tok_kind, home_kind, kind, ref in (
-                (r == n, TOK_UP, HOME_UP, UP, ups), (r == 3 - n, TOK_DOWN, HOME_DOWN, DOWN, dns)
+            for at_n, tok_kind, home_kind, kind, ref, kind2, ref2 in (
+                (r == n, TOK_UP, HOME_UP, UP, ups, UP2, ups2),
+                (r == 3 - n, TOK_DOWN, HOME_DOWN, DOWN, dns, DOWN2, dns2),
             ):
                 all_gone(tok_kind, x_all.at[pl.ds(0, n + 1)], at_n)
                 all_gone(home_kind, x_home.at[pl.ds(0, (n + 1) * tb)], at_n)
-                all_gone(kind, ref.at[pl.ds(0, (3 - n) * CHUNKS)], at_n)
+                all_gone(kind, ref.at[pl.ds(0, (3 - n) * LAST)], at_n)
+                all_gone(kind2, ref2.at[pl.ds(0, (3 - n) * 2)], at_n)
         all_gone(GI, x_all.at[0, pl.ds(0, 3 * CHUNKS * tl)])
         all_gone(GW, g_all.at[pl.ds(0, (6 * LAST + 5) * ic // 8)])
 
@@ -628,7 +658,8 @@
     ol = weight.shape[1]
     tb, ic = 4 * tl, il // (4 * CHUNKS)
     dma = pltpu.SemaphoreType.DMA
-    code = pltpu.VMEM((3 * CHUNKS, tb + GROUP, ic), BF16)
+    code = pltpu.VMEM((3 * LAST, tb + GROUP, ic), BF16)
+    code2 = pltpu.VMEM((6, tb + GROUP, ic // 2), BF16)
     anywhere = pl.BlockSpec(memory_space=pl.ANY)
     return store(*pl.pallas_call(
         kernel,
@@ -647,10 +678,10 @@
             pltpu.VMEM((CHUNKS, 4 * tb, ic), F32),
             pltpu.VMEM((CHUNKS, ic, 4 * ol), BF16),
             pltpu.VMEM((CHUNKS, tb, ic), BF16),
-            code, code, code, code,
+            code, code, code, code, code2, code2, code2, code2,
             pltpu.VMEM((4 * tb, ic // 2), BF16), pltpu.SemaphoreType.REGULAR((3,)),
             dma((2,)), dma((4,)), dma((4,)), dma((4,)), dma((4,)), dma((CHUNKS + 1,)), dma((CHUNKS,)),
-            dma((CHUNKS + 1, 4)), dma((3 * CHUNKS,)), dma((3 * CHUNKS,)), dma((2,)), dma((16,)),
+            dma((CHUNKS + 1, 4)), dma((3 * CHUNKS + 3,)), dma((3 * CHUNKS + 3,)), dma((2,)), dma((18,)),
         ],
         compiler_params=pltpu.CompilerParams(
             collective_id=0, has_side_effects=True, vmem_limit_bytes=46 * 2**20

time: 142 us -> 140 us (0.986)
  the two profiles are of different devices: /device:TPU:0 before, /device:TPU:21 now
where the time goes in v5:
time: 140 us; the launch traced here: 138 us
  Pallas kernels  138 us (99%)
    pallas_call x1, Pallas kernels, per_device_kernel(): pl.pallas_call(kernel, out_shape=(jax.ShapeDtypeStruct(tokens.shape, BF16...  135 us

profile of v5, /device:TPU:21, one launch (start us, length us, event | category | flops | bytes accessed | tf_op | source)
XLA Modules:
  0.0 138.5 jit_solution(3774266774368494996)
XLA Ops:
  0.6 135.3 %shard_map.50 = (bf16[128,4096]{1,0:T(8,128)(2,1)S(1)}, bf16[4096,512]{1,0:T(8,128)(2,1)S(1)}) custom-call(bf16[128,4096]{1,0:T(8,128)(2,1)} %tok.1, bf16[4096,512]{1,0:T(8,128)(2,1)} %w.1, bf16[512,1024]{1,0:T(8,128)(2,1)} %g.1), custom_call_target="tpu_custom_call" | custom-call | tf_op jit(solution)/shard_map/pallas_call | solution.py:664
  135.9 2.4 %shard_map.51 = (bf16[128,4096]{1,0:T(8,128)(2,1)}, bf16[4096,512]{1,0:T(8,128)(2,1)}) custom-call(bf16[128,4096]{1,0:T(8,128)(2,1)S(1)} %get-tuple-element.4.gi_in, bf16[4096,512]{1,0:T(8,128)(2,1)S(1)} %get-tuple-element.5.gw_in), custom_call_target="tpu_custom_call" | custom-call | tf_op jit(solution)/shard_map/pallas_call | solution.py:643

commit v6 on v5

--- a/solution.py
+++ b/solution.py
@@ -209,18 +209,25 @@
     last = 1 + r % 2
     order = [near, 6 - r - near - last, last, r]
 
-    def spread(n):
+    def landed(n):
+        s = order[n]
+        arrived(g_unit(s, d, c), g_z.at[s])
+
+    def spread_over(n):
         s = order[n]
         unit = g_unit(s, d, c)
-        arrived(unit, g_z.at[s])
         send(unit, unit, Y, g_y.at[s], {"depth": other})
-        if n < 3:
-            spread_across(n)
 
     def spread_across(n):
         s = order[n]
         unit = g_unit(s, d, c)
         send(unit, unit, X, g_x.at[s], {"col": across})
+
+    def spread(n):
+        landed(n)
+        spread_over(n)
+        if n < 3:
+            spread_across(n)
 
     def crossed(n):
         s = order[n]
@@ -465,8 +472,12 @@
         run("w_in%d" % j, weight_in, j)
         run("input%d" % j, multiply_input, j)
 
-    def mw(j):
-        run("pass%d_3" % j, pass_tokens, j, 3)
+    def mw(j, cond=None):
+        if cond is not inner:
+            run("pass%d_3" % j, pass_tokens, j, 3)
+        if cond is not None:
+            pl.when(cond)(lambda: run("weight%d" % j, multiply_weight, j))
+            return
         run("weight%d" % j, multiply_weight if j < LAST else multiply_weight_last, *([j] if j < LAST else []))
 
     def lv(j, n, which=None):
@@ -505,8 +516,10 @@
     run("spread3", spread, 3)
     run("mid1", pass_mid, 1)
     run("own1", own_tokens_on, 1)
-    for n in range(3):
-        run("spread%d" % n, spread, n)
+    run("spread0", spread, 0)
+    run("spread1", spread, 1)
+    run("landed2", landed, 2)
+    spread_across(2)
     spread_across(3)
     for j in range(1, CHUNKS):
         send_weight(j)
@@ -515,6 +528,7 @@
     run("own3", own_tokens_on, 3)
     run("own4", own_tokens_on, 4)
     run("crossed0", crossed, 0)
+    spread_over(2)
     run("crossed1", crossed, 1)
     ps(1, 1)
     run("crossed2", crossed, 2)
@@ -547,6 +561,7 @@
     for n in range(3):
         l0(2, n)
     l1(1, 0)
+    mw(1, inner)
     l2(0, 0)
     l1(1, 1)
     l2(0, 1)
@@ -554,7 +569,7 @@
     l1(1, 2)
     ps(3, 2)
     ps(4, 2)
-    mw(1)
+    mw(1, outer)
     mi(3)
     for p in (LAST, LAST + 1):
         for n in range(3):

time: 140 us -> 140 us (level)
  no operation moved by 1% of the time
where the time goes in v6:
time: 140 us; the launch traced here: 138 us
  Pallas kernels  138 us (99%)
    pallas_call x1, Pallas kernels, per_device_kernel(): pl.pallas_call(kernel, out_shape=(jax.ShapeDtypeStruct(tokens.shape, BF16...  135 us

profile of v6, /device:TPU:21, one launch (start us, length us, event | category | flops | bytes accessed | tf_op | source)
XLA Modules:
  0.0 138.5 jit_solution(1887522889379811176)
XLA Ops:
  0.6 135.3 %shard_map.50 = (bf16[128,4096]{1,0:T(8,128)(2,1)S(1)}, bf16[4096,512]{1,0:T(8,128)(2,1)S(1)}) custom-call(bf16[128,4096]{1,0:T(8,128)(2,1)} %tok.1, bf16[4096,512]{1,0:T(8,128)(2,1)} %w.1, bf16[512,1024]{1,0:T(8,128)(2,1)} %g.1), custom_call_target="tpu_custom_call" | custom-call | tf_op jit(solution)/shard_map/pallas_call | solution.py:679
  135.9 2.4 %shard_map.51 = (bf16[128,4096]{1,0:T(8,128)(2,1)}, bf16[4096,512]{1,0:T(8,128)(2,1)}) custom-call(bf16[128,4096]{1,0:T(8,128)(2,1)S(1)} %get-tuple-element.4.gi_in, bf16[4096,512]{1,0:T(8,128)(2,1)S(1)} %get-tuple-element.5.gw_in), custom_call_target="tpu_custom_call" | custom-call | tf_op jit(solution)/shard_map/pallas_call | solution.py:658
